TPU v7x, 32 devices: a whole 2x2x4 slice. The times are simulated.
32 devices in a mesh: level: 2 (over core), gx: 4 (over y, x), yz: 4 (over z).
Axes of the slice: x: 2, y: 2, z: 4, core: 2. Of those that a mesh axis runs over, the one named last changes fastest.
Arguments:
- init_field: float32 [128, 64, 256], P('gx', 'yz'), may hold values from -6 to 6
- source: float32 [128, 64, 256], P('gx', 'yz'), may hold values from -4 to 4
- damping: float32 [128, 64, 256], P('gx', 'yz'), may hold values from 0.05 to 2
Outputs:
- final_states: float32 [2, 128, 64, 256], P('level', 'gx', 'yz')
All inputs are finite; a program needn't handle non-finite values.
Results may differ from a plain program's by a relative error of at most 0.0001.
Values sent between devices are 32-bit elements; how exact they have to be, the bound alone decides.
A program may use at most 64 MiB of HBM per device.

v0:
```python
import jax
import jax.numpy as jnp
from jax import lax
from jax.sharding import PartitionSpec as P

STEPS = 3
ITERS = 3
diffusion_number = 1.0


def extended(cells, sides, width):
    for axis, dim in sides:
        count = lax.axis_size(axis)
        ends = count - 1
        head = lax.slice_in_dim(cells, 0, width, axis=dim)
        tail = lax.slice_in_dim(cells, cells.shape[dim] - width, cells.shape[dim], axis=dim)
        cells = jnp.concatenate(
            [
                lax.ppermute(tail, axis, [(i, (i + 1) % count) for i in range(ends)]),
                cells,
                lax.ppermute(head, axis, [((i + 1) % count, i) for i in range(ends)]),
            ],
            axis=dim,
        )
    return cells


def passed_along(block, axis, distance):
    devices = range(lax.axis_size(axis))
    route = [(i - distance, i) for i in devices if i - distance in devices]
    return lax.ppermute(block, axis, route)


def stencil_from(padded, field, damping):
    beside = padded[2:, 1:-1, :] + padded[:-2, 1:-1, :]
    beside = beside + padded[1:-1, 2:, :] + padded[1:-1, :-2, :]
    zero_plane = jnp.zeros_like(field[:, :, :1])
    beside = beside + jnp.concatenate([field[:, :, 1:], zero_plane], axis=2)
    beside = beside + jnp.concatenate([zero_plane, field[:, :, :-1]], axis=2)
    return damping * field + diffusion_number * (6.0 * field - beside)


def operate(field, damping):
    padded = extended(field, (("gx", 0), ("yz", 1)), 1)
    return field + stencil_from(padded, field, damping)


def two_products(resid, image):
    return lax.psum((jnp.sum(resid * resid), jnp.sum(resid * image)), ("gx", "yz"))


def solve(target, guess, damping):
    answer = guess
    resid = target - operate(answer, damping)
    image = operate(resid, damping)
    norm_now, product = two_products(resid, image)
    alpha = norm_now / product
    direction, along = (resid, image)
    for step in range(ITERS):
        answer = answer + alpha * direction
        resid = resid - alpha * along
        if step + 1 < ITERS:
            image = operate(resid, damping)
            norm_next, product = two_products(resid, image)
            ratio = norm_next / norm_now
            alpha = norm_next / (product - ratio * norm_next / alpha)
            direction = resid + ratio * direction
            along = image + ratio * along
            norm_now = norm_next
    return answer


def per_device(init_field, source, damping):
    upper = lax.axis_index("level") == 1
    state = init_field
    older = jnp.where(upper, init_field, jnp.zeros_like(init_field))
    for rounds in range(STEPS + 1):
        if rounds == 0:
            extra = jnp.zeros_like(init_field)
        else:
            incoming = passed_along(state, "level", 1)
            change = incoming - older
            older = incoming
            padded = extended(change, (("gx", 0), ("yz", 1)), 1)
            extra = 0.5 * stencil_from(padded, change, damping)
        fresh = solve(state + source + extra, state, damping)
        if rounds == 0:
            state = jnp.where(upper, state, fresh)
        elif rounds == STEPS:
            state = jnp.where(upper, fresh, state)
        else:
            state = fresh
    return state[None]


def solution(mesh):
    in_specs = (P("gx", "yz", None), P("gx", "yz", None), P("gx", "yz", None))
    out_specs = P("level", "gx", "yz", None)
    return jax.shard_map(
        per_device, mesh=mesh, in_specs=in_specs, out_specs=out_specs, check_vma=False
    )
```

profile of v0, /device:TPU:0, one launch (start us, length us, event | category | flops | bytes accessed | tf_op | source)
XLA Modules:
  0.0 858.0 jit_solution(10552199963659555347)
XLA Ops:
  0.7 4.9 collective-permute-start.1
  38.3 40.1 %all-reduce.49 = (f32[]{:T(128)}, f32[]{:T(128)}) all-reduce(f32[]{:T(128)} %get-tuple-element.28, f32[]{:T(128)} %get-tuple-element.27), channel_id=1, replica_groups=mesh['level'=2,'gx'=4,'yz'=4] {'gx','yz'}, use_global_device_ids=true, to_apply=%region_1.2 | all-reduce | flops 2 | bytes 16 | tf_op jit(solution)/shard_map/psum | solution.py:49
  83.3 8.2 collective-permute-done.8
  100.9 39.7 %all-reduce.48 = (f32[]{:T(128)}, f32[]{:T(128)}) all-reduce(f32[]{:T(128)} %get-tuple-element.26, f32[]{:T(128)} %get-tuple-element.25), channel_id=1, replica_groups=mesh['level'=2,'gx'=4,'yz'=4] {'gx','yz'}, use_global_device_ids=true, to_apply=%region_5.6 | all-reduce | flops 2 | bytes 16 | tf_op jit(solution)/shard_map/psum | solution.py:49
  149.0 5.5 collective-permute-done.12
  163.2 39.7 %all-reduce.47 = (f32[]{:T(128)}, f32[]{:T(128)}) all-reduce(f32[]{:T(128)} %get-tuple-element.24, f32[]{:T(128)} %get-tuple-element.23), channel_id=1, replica_groups=mesh['level'=2,'gx'=4,'yz'=4] {'gx','yz'}, use_global_device_ids=true, to_apply=%region_9.10 | all-reduce | flops 2 | bytes 16 | tf_op jit(solution)/shard_map/psum | solution.py:49
  212.1 7.1 collective-permute-start.18
  234.9 5.4 collective-permute-start.26
  241.8 5.1 collective-permute-done.25
  255.8 39.8 %all-reduce.46 = (f32[]{:T(128)}, f32[]{:T(128)}) all-reduce(f32[]{:T(128)} %get-tuple-element.22, f32[]{:T(128)} %get-tuple-element.21), channel_id=1, replica_groups=mesh['level'=2,'gx'=4,'yz'=4] {'gx','yz'}, use_global_device_ids=true, to_apply=%region_13.14 | all-reduce | flops 2 | bytes 16 | tf_op jit(solution)/shard_map/psum | solution.py:49
  299.6 8.9 %collective-permute-done.29 = f32[1,16,256]{2,1,0:T(8,128)S(1)} collective-permute-done((f32[1,16,256]{2,1,0:T(8,128)S(1)}, f32[1,16,256]{2,1,0:T(8,128)S(1)}, u32[]{:S(2)}, u32[]{:S(2)}) %collective-permute-start.29) | collective-permute-done | bytes 16416 | tf_op jit(solution)/shard_map/ppermute | solution.py:21
  317.9 39.7 %all-reduce.45 = (f32[]{:T(128)}, f32[]{:T(128)}) all-reduce(f32[]{:T(128)} %get-tuple-element.20, f32[]{:T(128)} %get-tuple-element.19), channel_id=1, replica_groups=mesh['level'=2,'gx'=4,'yz'=4] {'gx','yz'}, use_global_device_ids=true, to_apply=%region_17.18 | all-reduce | flops 2 | bytes 16 | tf_op jit(solution)/shard_map/psum | solution.py:49
  366.0 5.5 collective-permute-done.33
  380.0 39.7 %all-reduce.44 = (f32[]{:T(128)}, f32[]{:T(128)}) all-reduce(f32[]{:T(128)} %get-tuple-element.18, f32[]{:T(128)} %get-tuple-element.17), channel_id=1, replica_groups=mesh['level'=2,'gx'=4,'yz'=4] {'gx','yz'}, use_global_device_ids=true, to_apply=%region_21.22 | all-reduce | flops 2 | bytes 16 | tf_op jit(solution)/shard_map/psum | solution.py:49
  428.8 7.2 collective-permute-start.39
  444.6 4.9 collective-permute-start.41
  451.7 5.4 collective-permute-start.47
  458.5 5.1 collective-permute-done.46
  465.0 4.9 collective-permute-start.49
  472.6 39.8 %all-reduce.43 = (f32[]{:T(128)}, f32[]{:T(128)}) all-reduce(f32[]{:T(128)} %get-tuple-element.16, f32[]{:T(128)} %get-tuple-element.15), channel_id=1, replica_groups=mesh['level'=2,'gx'=4,'yz'=4] {'gx','yz'}, use_global_device_ids=true, to_apply=%region_25.26 | all-reduce | flops 2 | bytes 16 | tf_op jit(solution)/shard_map/psum | solution.py:49
  516.4 8.9 %collective-permute-done.50 = f32[1,16,256]{2,1,0:T(8,128)S(1)} collective-permute-done((f32[1,16,256]{2,1,0:T(8,128)S(1)}, f32[1,16,256]{2,1,0:T(8,128)S(1)}, u32[]{:S(2)}, u32[]{:S(2)}) %collective-permute-start.50) | collective-permute-done | bytes 16416 | tf_op jit(solution)/shard_map/ppermute | solution.py:21
  534.7 39.8 %all-reduce.42 = (f32[]{:T(128)}, f32[]{:T(128)}) all-reduce(f32[]{:T(128)} %get-tuple-element.14, f32[]{:T(128)} %get-tuple-element.13), channel_id=1, replica_groups=mesh['level'=2,'gx'=4,'yz'=4] {'gx','yz'}, use_global_device_ids=true, to_apply=%region_29.30 | all-reduce | flops 2 | bytes 16 | tf_op jit(solution)/shard_map/psum | solution.py:49
  582.8 5.4 collective-permute-done.54
  596.9 39.7 %all-reduce.41 = (f32[]{:T(128)}, f32[]{:T(128)}) all-reduce(f32[]{:T(128)} %get-tuple-element.12, f32[]{:T(128)} %get-tuple-element.11), channel_id=1, replica_groups=mesh['level'=2,'gx'=4,'yz'=4] {'gx','yz'}, use_global_device_ids=true, to_apply=%region_33.34 | all-reduce | flops 2 | bytes 16 | tf_op jit(solution)/shard_map/psum | solution.py:49
  644.9 7.2 collective-permute-start.60
  667.8 5.4 collective-permute-start.68
  674.7 5.1 collective-permute-done.67
  688.6 39.8 %all-reduce.40 = (f32[]{:T(128)}, f32[]{:T(128)}) all-reduce(f32[]{:T(128)} %get-tuple-element.10, f32[]{:T(128)} %get-tuple-element.9), channel_id=1, replica_groups=mesh['level'=2,'gx'=4,'yz'=4] {'gx','yz'}, use_global_device_ids=true, to_apply=%region_37.38 | all-reduce | flops 2 | bytes 16 | tf_op jit(solution)/shard_map/psum | solution.py:49
  732.7 8.9 %collective-permute-done.71 = f32[1,16,256]{2,1,0:T(8,128)S(1)} collective-permute-done((f32[1,16,256]{2,1,0:T(8,128)S(1)}, f32[1,16,256]{2,1,0:T(8,128)S(1)}, u32[]{:S(2)}, u32[]{:S(2)}) %collective-permute-start.71) | collective-permute-done | bytes 16416 | tf_op jit(solution)/shard_map/ppermute | solution.py:21
  751.0 39.7 %all-reduce.39 = (f32[]{:T(128)}, f32[]{:T(128)}) all-reduce(f32[]{:T(128)} %get-tuple-element.8, f32[]{:T(128)} %get-tuple-element.7), channel_id=1, replica_groups=mesh['level'=2,'gx'=4,'yz'=4] {'gx','yz'}, use_global_device_ids=true, to_apply=%region_41.42 | all-reduce | flops 2 | bytes 16 | tf_op jit(solution)/shard_map/psum | solution.py:49
  799.2 5.5 collective-permute-done.75
  813.3 39.7 %all-reduce.38 = (f32[]{:T(128)}, f32[]{:T(128)}) all-reduce(f32[]{:T(128)} %get-tuple-element.6, f32[]{:T(128)} %get-tuple-element.5), channel_id=1, replica_groups=mesh['level'=2,'gx'=4,'yz'=4] {'gx','yz'}, use_global_device_ids=true, to_apply=%region_45.46 | all-reduce | flops 2 | bytes 16 | tf_op jit(solution)/shard_map/psum | solution.py:49
  (249 shorter events, 216.7 us)
Async XLA Ops:
  81.9 9.6 %collective-permute-start.8 = (f32[1,16,256]{2,1,0:T(8,128)S(1)}, f32[1,16,256]{2,1,0:T(8,128)S(1)}, u32[]{:S(2)}, u32[]{:S(2)}) collective-permute-start(f32[1,16,256]{2,1,0:T(8,128)S(1)} %get-tuple-element.164), channel_id=1, source_target_pairs={{4,0},{8,4},{12,8},{5,1},{9,5},{13,9},{6,2},{10,6},{14,10},{7,3},{... | collective-permute-start | bytes 49160 | tf_op jit(solution)/shard_map/ppermute | solution.py:21
  147.6 7.0 collective-permute-start.12
  208.4 12.0 %collective-permute-start.22 = (f32[1,16,256]{2,1,0:T(8,128)S(1)}, f32[1,16,256]{2,1,0:T(8,128)S(1)}, u32[]{:S(2)}, u32[]{:S(2)}) collective-permute-start(f32[1,16,256]{2,1,0:T(8,128)S(1)} %get-tuple-element.157), channel_id=1, source_target_pairs={{0,4},{4,8},{8,12},{1,5},{5,9},{9,13},{2,6},{6,10},{10,14},{3,7},{... | collective-permute-start | bytes 49160 | tf_op jit(solution)/shard_map/ppermute | solution.py:19
  209.7 10.7 %collective-permute-start.21 = (f32[1,16,256]{2,1,0:T(8,128)S(1)}, f32[1,16,256]{2,1,0:T(8,128)S(1)}, u32[]{:S(2)}, u32[]{:S(2)}) collective-permute-start(f32[1,16,256]{2,1,0:T(8,128)S(1)} %get-tuple-element.158), channel_id=1, source_target_pairs={{4,0},{8,4},{12,8},{5,1},{9,5},{13,9},{6,2},{10,6},{14,10},{7,3},{... | collective-permute-start | bytes 49160 | tf_op jit(solution)/shard_map/ppermute | solution.py:21
  212.1 14.3 %collective-permute-start.18 = (f32[1,16,256]{2,1,0:T(8,128)S(1)}, f32[1,16,256]{2,1,0:T(8,128)S(1)}, u32[]{:S(2)}, u32[]{:S(2)}) collective-permute-start(f32[1,16,256]{2,1,0:T(8,128)S(1)} %get-tuple-element.155), channel_id=1, source_target_pairs={{0,4},{4,8},{8,12},{1,5},{5,9},{9,13},{2,6},{6,10},{10,14},{3,7},{... | collective-permute-start | bytes 49160 | tf_op jit(solution)/shard_map/ppermute | solution.py:19
  219.2 7.2 collective-permute-start.17
  220.5 12.2 %collective-permute-start.23 = (f32[34,1,256]{2,1,0:T(1,128)S(1)}, f32[34,1,256]{2,1,0:T(1,128)S(1)}, u32[]{:S(2)}, u32[]{:S(2)}) collective-permute-start(f32[34,1,256]{2,1,0:T(1,128)S(1)} %get-tuple-element.89), channel_id=1, source_target_pairs={{1,0},{2,1},{3,2},{5,4},{6,5},{7,6},{9,8},{10,9},{11,10},{13,12},{... | collective-permute-start | bytes 104456 | tf_op jit(solution)/shard_map/ppermute | solution.py:21
  221.8 10.9 %collective-permute-start.24 = (f32[34,1,256]{2,1,0:T(1,128)S(1)}, f32[34,1,256]{2,1,0:T(1,128)S(1)}, u32[]{:S(2)}, u32[]{:S(2)}) collective-permute-start(f32[34,1,256]{2,1,0:T(1,128)S(1)} %get-tuple-element.90), channel_id=1, source_target_pairs={{0,1},{1,2},{2,3},{4,5},{5,6},{6,7},{8,9},{9,10},{10,11},{12,13},{... | collective-permute-start | bytes 104456 | tf_op jit(solution)/shard_map/ppermute | solution.py:19
  234.9 6.9 collective-permute-start.26
  240.3 6.5 collective-permute-start.25
  298.2 10.3 %collective-permute-start.29 = (f32[1,16,256]{2,1,0:T(8,128)S(1)}, f32[1,16,256]{2,1,0:T(8,128)S(1)}, u32[]{:S(2)}, u32[]{:S(2)}) collective-permute-start(f32[1,16,256]{2,1,0:T(8,128)S(1)} %get-tuple-element.144), channel_id=1, source_target_pairs={{4,0},{8,4},{12,8},{5,1},{9,5},{13,9},{6,2},{10,6},{14,10},{7,3},{... | collective-permute-start | bytes 49160 | tf_op jit(solution)/shard_map/ppermute | solution.py:21
  364.5 6.9 collective-permute-start.33
  425.0 12.3 %collective-permute-start.43 = (f32[1,16,256]{2,1,0:T(8,128)S(1)}, f32[1,16,256]{2,1,0:T(8,128)S(1)}, u32[]{:S(2)}, u32[]{:S(2)}) collective-permute-start(f32[1,16,256]{2,1,0:T(8,128)S(1)} %get-tuple-element.137), channel_id=1, source_target_pairs={{0,4},{4,8},{8,12},{1,5},{5,9},{9,13},{2,6},{6,10},{10,14},{3,7},{... | collective-permute-start | bytes 49160 | tf_op jit(solution)/shard_map/ppermute | solution.py:19
  426.3 11.0 %collective-permute-start.42 = (f32[1,16,256]{2,1,0:T(8,128)S(1)}, f32[1,16,256]{2,1,0:T(8,128)S(1)}, u32[]{:S(2)}, u32[]{:S(2)}) collective-permute-start(f32[1,16,256]{2,1,0:T(8,128)S(1)} %get-tuple-element.138), channel_id=1, source_target_pairs={{4,0},{8,4},{12,8},{5,1},{9,5},{13,9},{6,2},{10,6},{14,10},{7,3},{... | collective-permute-start | bytes 49160 | tf_op jit(solution)/shard_map/ppermute | solution.py:21
  428.8 14.4 %collective-permute-start.39 = (f32[1,16,256]{2,1,0:T(8,128)S(1)}, f32[1,16,256]{2,1,0:T(8,128)S(1)}, u32[]{:S(2)}, u32[]{:S(2)}) collective-permute-start(f32[1,16,256]{2,1,0:T(8,128)S(1)} %get-tuple-element.135), channel_id=1, source_target_pairs={{0,4},{4,8},{8,12},{1,5},{5,9},{9,13},{2,6},{6,10},{10,14},{3,7},{... | collective-permute-start | bytes 49160 | tf_op jit(solution)/shard_map/ppermute | solution.py:19
  435.9 7.2 collective-permute-start.38
  437.3 12.3 %collective-permute-start.44 = (f32[34,1,256]{2,1,0:T(1,128)S(1)}, f32[34,1,256]{2,1,0:T(1,128)S(1)}, u32[]{:S(2)}, u32[]{:S(2)}) collective-permute-start(f32[34,1,256]{2,1,0:T(1,128)S(1)} %get-tuple-element.79), channel_id=1, source_target_pairs={{1,0},{2,1},{3,2},{5,4},{6,5},{7,6},{9,8},{10,9},{11,10},{13,12},{... | collective-permute-start | bytes 104456 | tf_op jit(solution)/shard_map/ppermute | solution.py:21
  438.6 11.0 %collective-permute-start.45 = (f32[34,1,256]{2,1,0:T(1,128)S(1)}, f32[34,1,256]{2,1,0:T(1,128)S(1)}, u32[]{:S(2)}, u32[]{:S(2)}) collective-permute-start(f32[34,1,256]{2,1,0:T(1,128)S(1)} %get-tuple-element.80), channel_id=1, source_target_pairs={{0,1},{1,2},{2,3},{4,5},{5,6},{6,7},{8,9},{9,10},{10,11},{12,13},{... | collective-permute-start | bytes 104456 | tf_op jit(solution)/shard_map/ppermute | solution.py:19
  451.7 6.9 collective-permute-start.47
  457.1 6.5 collective-permute-start.46
  515.0 10.4 %collective-permute-start.50 = (f32[1,16,256]{2,1,0:T(8,128)S(1)}, f32[1,16,256]{2,1,0:T(8,128)S(1)}, u32[]{:S(2)}, u32[]{:S(2)}) collective-permute-start(f32[1,16,256]{2,1,0:T(8,128)S(1)} %get-tuple-element.124), channel_id=1, source_target_pairs={{4,0},{8,4},{12,8},{5,1},{9,5},{13,9},{6,2},{10,6},{14,10},{7,3},{... | collective-permute-start | bytes 49160 | tf_op jit(solution)/shard_map/ppermute | solution.py:21
  581.4 6.9 collective-permute-start.54
  641.8 11.6 %collective-permute-start.64 = (f32[1,16,256]{2,1,0:T(8,128)S(1)}, f32[1,16,256]{2,1,0:T(8,128)S(1)}, u32[]{:S(2)}, u32[]{:S(2)}) collective-permute-start(f32[1,16,256]{2,1,0:T(8,128)S(1)} %get-tuple-element.117), channel_id=1, source_target_pairs={{0,4},{4,8},{8,12},{1,5},{5,9},{9,13},{2,6},{6,10},{10,14},{3,7},{... | collective-permute-start | bytes 49160 | tf_op jit(solution)/shard_map/ppermute | solution.py:19
  643.1 10.3 %collective-permute-start.63 = (f32[1,16,256]{2,1,0:T(8,128)S(1)}, f32[1,16,256]{2,1,0:T(8,128)S(1)}, u32[]{:S(2)}, u32[]{:S(2)}) collective-permute-start(f32[1,16,256]{2,1,0:T(8,128)S(1)} %get-tuple-element.118), channel_id=1, source_target_pairs={{4,0},{8,4},{12,8},{5,1},{9,5},{13,9},{6,2},{10,6},{14,10},{7,3},{... | collective-permute-start | bytes 49160 | tf_op jit(solution)/shard_map/ppermute | solution.py:21
  644.9 14.4 %collective-permute-start.60 = (f32[1,16,256]{2,1,0:T(8,128)S(1)}, f32[1,16,256]{2,1,0:T(8,128)S(1)}, u32[]{:S(2)}, u32[]{:S(2)}) collective-permute-start(f32[1,16,256]{2,1,0:T(8,128)S(1)} %get-tuple-element.115), channel_id=1, source_target_pairs={{0,4},{4,8},{8,12},{1,5},{5,9},{9,13},{2,6},{6,10},{10,14},{3,7},{... | collective-permute-start | bytes 49160 | tf_op jit(solution)/shard_map/ppermute | solution.py:19
  652.1 7.2 collective-permute-start.59
  653.4 12.2 %collective-permute-start.65 = (f32[34,1,256]{2,1,0:T(1,128)S(1)}, f32[34,1,256]{2,1,0:T(1,128)S(1)}, u32[]{:S(2)}, u32[]{:S(2)}) collective-permute-start(f32[34,1,256]{2,1,0:T(1,128)S(1)} %get-tuple-element.69), channel_id=1, source_target_pairs={{1,0},{2,1},{3,2},{5,4},{6,5},{7,6},{9,8},{10,9},{11,10},{13,12},{... | collective-permute-start | bytes 104456 | tf_op jit(solution)/shard_map/ppermute | solution.py:21
  654.7 10.9 %collective-permute-start.66 = (f32[34,1,256]{2,1,0:T(1,128)S(1)}, f32[34,1,256]{2,1,0:T(1,128)S(1)}, u32[]{:S(2)}, u32[]{:S(2)}) collective-permute-start(f32[34,1,256]{2,1,0:T(1,128)S(1)} %get-tuple-element.70), channel_id=1, source_target_pairs={{0,1},{1,2},{2,3},{4,5},{5,6},{6,7},{8,9},{9,10},{10,11},{12,13},{... | collective-permute-start | bytes 104456 | tf_op jit(solution)/shard_map/ppermute | solution.py:19
  667.8 6.9 collective-permute-start.68
  673.2 6.5 collective-permute-start.67
  731.3 10.4 %collective-permute-start.71 = (f32[1,16,256]{2,1,0:T(8,128)S(1)}, f32[1,16,256]{2,1,0:T(8,128)S(1)}, u32[]{:S(2)}, u32[]{:S(2)}) collective-permute-start(f32[1,16,256]{2,1,0:T(8,128)S(1)} %get-tuple-element.104), channel_id=1, source_target_pairs={{4,0},{8,4},{12,8},{5,1},{9,5},{13,9},{6,2},{10,6},{14,10},{7,3},{... | collective-permute-start | bytes 49160 | tf_op jit(solution)/shard_map/ppermute | solution.py:21
  797.7 6.9 collective-permute-start.75
  (57 other events, 304.7 us)
where the time goes:
time: 861 us; the launch traced here: 858 us
  blocking collectives  477 us (55%)
  starting transfers between devices  204 us (24%)
  waiting for transfers between devices  103 us (12%)
  between operations  39.6 us (5%)
  other arithmetic  27.4 us (3%)
    psum x12, blocking collectives, two_products(): lax.psum((jnp.sum(resid * resid), jnp.sum(resid * image)), ('gx', 'yz'))  477 us
    ppermute x38, starting transfers between devices, extended(): lax.ppermute(tail, axis, [(i, (i + 1) % count) for i in range(ends)])  150 us
    ppermute x38, waiting for transfers between devices, extended(): lax.ppermute(head, axis, [((i + 1) % count, i) for i in range(ends)])  79.6 us
    ppermute x38, starting transfers between devices, extended(): lax.ppermute(head, axis, [((i + 1) % count, i) for i in range(ends)])  49.4 us
    ppermute x38, waiting for transfers between devices, extended(): lax.ppermute(tail, axis, [(i, (i + 1) % count) for i in range(ends)])  23.4 us
  transfers between devices with their start and end apart: 79, of which 42 were waited for; matrix products, arithmetic and copies ran while one was open for 1% of the time, Pallas kernels for 0%

commit v1 on v0

--- a/solution.py
+++ b/solution.py
@@ -46,7 +46,10 @@
 
 
 def two_products(resid, image):
-    return lax.psum((jnp.sum(resid * resid), jnp.sum(resid * image)), ("gx", "yz"))
+    report_target = lambda shard_in, axis_name, peer_axis: lax.psum(
+        lax.psum(shard_in, axis_name), peer_axis
+    )
+    return report_target((jnp.sum(resid * resid), jnp.sum(resid * image)), "yz", "gx")
 
 
 def solve(target, guess, damping):

time: 861 us -> 641 us (0.74)
  blocking collectives: 477 us -> 272 us
  waiting for transfers between devices: 103 us -> 88.5 us
    psum x12 -> x24, blocking collectives: 477 us -> 272 us  [the longest x12 141 us: two_products(): lax.psum(shard_in, axis_name)]
    ppermute x38, waiting for transfers between devices: 79.6 us -> 64.9 us  [extended(): lax.ppermute(head, axis, [((i + 1) % count, i) for i in range(ends)])]
where the time goes in v1:
time: 641 us; the launch traced here: 637 us
  blocking collectives  272 us (42%)
  starting transfers between devices  203 us (32%)
  waiting for transfers between devices  88.5 us (14%)
  between operations  39.3 us (6%)
  other arithmetic  27.1 us (4%)
  local copies, waits for them, and re-layouts  7.39 us (1%)
    ppermute x38, starting transfers between devices, extended(): lax.ppermute(tail, axis, [(i, (i + 1) % count) for i in range(ends)])  150 us
    psum x12, blocking collectives, two_products(): lax.psum(shard_in, axis_name)  141 us
    psum x12, blocking collectives, two_products(): lax.psum(lax.psum(shard_in, axis_name), peer_axis)  131 us
    ppermute x38, waiting for transfers between devices, extended(): lax.ppermute(head, axis, [((i + 1) % count, i) for i in range(ends)])  64.9 us
    ppermute x38, starting transfers between devices, extended(): lax.ppermute(head, axis, [((i + 1) % count, i) for i in range(ends)])  49.5 us
    ppermute x38, waiting for transfers between devices, extended(): lax.ppermute(tail, axis, [(i, (i + 1) % count) for i in range(ends)])  23.6 us
    reduce_sum x12, other arithmetic, two_products(): jnp.sum(resid * image)  16 us
  transfers between devices with their start and end apart: 79, of which 42 were waited for; matrix products, arithmetic and copies ran while one was open for 1% of the time, Pallas kernels for 0%

profile of v1, /device:TPU:0, one launch (start us, length us, event | category | flops | bytes accessed | tf_op | source)
XLA Modules:
  0.0 637.2 jit_solution(3748234381024883464)
XLA Ops:
  38.2 13.8 %all-reduce.49 = (f32[]{:T(128)}, f32[]{:T(128)}) all-reduce(f32[]{:T(128)} %get-tuple-element.28, f32[]{:T(128)} %get-tuple-element.27), channel_id=1, replica_groups=mesh['level'=2,'gx'=4,'yz'=4] {'yz'}, use_global_device_ids=true, to_apply=%region_1.2 | all-reduce | flops 2 | bytes 16 | tf_op jit(solution)/shard_map/psum | solution.py:50
  52.0 9.6 %all-reduce.61 = (f32[]{:T(128)}, f32[]{:T(128)}) all-reduce(f32[]{:T(128)} %get-tuple-element.51, f32[]{:T(128)} %get-tuple-element.52), channel_id=1, replica_groups=mesh['level'=2,'gx'=4,'yz'=4] {'gx'}, use_global_device_ids=true, to_apply=%region_2.3 | all-reduce | flops 2 | bytes 16 | tf_op jit(solution)/shard_map/psum | solution.py:49
  80.8 11.3 %all-reduce.48 = (f32[]{:T(128)}, f32[]{:T(128)}) all-reduce(f32[]{:T(128)} %get-tuple-element.26, f32[]{:T(128)} %get-tuple-element.25), channel_id=1, replica_groups=mesh['level'=2,'gx'=4,'yz'=4] {'yz'}, use_global_device_ids=true, to_apply=%region_7.8 | all-reduce | flops 2 | bytes 16 | tf_op jit(solution)/shard_map/psum | solution.py:50
  92.1 11.0 %all-reduce.60 = (f32[]{:T(128)}, f32[]{:T(128)}) all-reduce(f32[]{:T(128)} %get-tuple-element.49, f32[]{:T(128)} %get-tuple-element.50), channel_id=1, replica_groups=mesh['level'=2,'gx'=4,'yz'=4] {'gx'}, use_global_device_ids=true, to_apply=%region_8.9 | all-reduce | flops 2 | bytes 16 | tf_op jit(solution)/shard_map/psum | solution.py:49
  111.8 5.4 collective-permute-done.12
  125.8 11.3 %all-reduce.47 = (f32[]{:T(128)}, f32[]{:T(128)}) all-reduce(f32[]{:T(128)} %get-tuple-element.24, f32[]{:T(128)} %get-tuple-element.23), channel_id=1, replica_groups=mesh['level'=2,'gx'=4,'yz'=4] {'yz'}, use_global_device_ids=true, to_apply=%region_13.14 | all-reduce | flops 2 | bytes 16 | tf_op jit(solution)/shard_map/psum | solution.py:50
  137.0 11.0 %all-reduce.59 = (f32[]{:T(128)}, f32[]{:T(128)}) all-reduce(f32[]{:T(128)} %get-tuple-element.47, f32[]{:T(128)} %get-tuple-element.48), channel_id=1, replica_groups=mesh['level'=2,'gx'=4,'yz'=4] {'gx'}, use_global_device_ids=true, to_apply=%region_14.15 | all-reduce | flops 2 | bytes 16 | tf_op jit(solution)/shard_map/psum | solution.py:49
  157.5 5.7 collective-permute-start.18
  178.9 5.4 collective-permute-start.26
  199.8 12.2 %all-reduce.46 = (f32[]{:T(128)}, f32[]{:T(128)}) all-reduce(f32[]{:T(128)} %get-tuple-element.22, f32[]{:T(128)} %get-tuple-element.21), channel_id=1, replica_groups=mesh['level'=2,'gx'=4,'yz'=4] {'yz'}, use_global_device_ids=true, to_apply=%region_19.20 | all-reduce | flops 2 | bytes 16 | tf_op jit(solution)/shard_map/psum | solution.py:50
  212.0 11.0 %all-reduce.58 = (f32[]{:T(128)}, f32[]{:T(128)}) all-reduce(f32[]{:T(128)} %get-tuple-element.45, f32[]{:T(128)} %get-tuple-element.46), channel_id=1, replica_groups=mesh['level'=2,'gx'=4,'yz'=4] {'gx'}, use_global_device_ids=true, to_apply=%region_20.21 | all-reduce | flops 2 | bytes 16 | tf_op jit(solution)/shard_map/psum | solution.py:49
  227.5 5.4 collective-permute-done.29
  242.3 11.3 %all-reduce.45 = (f32[]{:T(128)}, f32[]{:T(128)}) all-reduce(f32[]{:T(128)} %get-tuple-element.20, f32[]{:T(128)} %get-tuple-element.19), channel_id=1, replica_groups=mesh['level'=2,'gx'=4,'yz'=4] {'yz'}, use_global_device_ids=true, to_apply=%region_25.26 | all-reduce | flops 2 | bytes 16 | tf_op jit(solution)/shard_map/psum | solution.py:50
  253.6 11.0 %all-reduce.57 = (f32[]{:T(128)}, f32[]{:T(128)}) all-reduce(f32[]{:T(128)} %get-tuple-element.43, f32[]{:T(128)} %get-tuple-element.44), channel_id=1, replica_groups=mesh['level'=2,'gx'=4,'yz'=4] {'gx'}, use_global_device_ids=true, to_apply=%region_26.27 | all-reduce | flops 2 | bytes 16 | tf_op jit(solution)/shard_map/psum | solution.py:49
  287.3 11.3 %all-reduce.44 = (f32[]{:T(128)}, f32[]{:T(128)}) all-reduce(f32[]{:T(128)} %get-tuple-element.18, f32[]{:T(128)} %get-tuple-element.17), channel_id=1, replica_groups=mesh['level'=2,'gx'=4,'yz'=4] {'yz'}, use_global_device_ids=true, to_apply=%region_31.32 | all-reduce | flops 2 | bytes 16 | tf_op jit(solution)/shard_map/psum | solution.py:50
  298.6 11.0 %all-reduce.56 = (f32[]{:T(128)}, f32[]{:T(128)}) all-reduce(f32[]{:T(128)} %get-tuple-element.41, f32[]{:T(128)} %get-tuple-element.42), channel_id=1, replica_groups=mesh['level'=2,'gx'=4,'yz'=4] {'gx'}, use_global_device_ids=true, to_apply=%region_32.33 | all-reduce | flops 2 | bytes 16 | tf_op jit(solution)/shard_map/psum | solution.py:49
  319.2 5.7 collective-permute-start.39
  340.8 5.4 collective-permute-start.47
  361.7 12.2 %all-reduce.43 = (f32[]{:T(128)}, f32[]{:T(128)}) all-reduce(f32[]{:T(128)} %get-tuple-element.16, f32[]{:T(128)} %get-tuple-element.15), channel_id=1, replica_groups=mesh['level'=2,'gx'=4,'yz'=4] {'yz'}, use_global_device_ids=true, to_apply=%region_37.38 | all-reduce | flops 2 | bytes 16 | tf_op jit(solution)/shard_map/psum | solution.py:50
  373.9 11.0 %all-reduce.55 = (f32[]{:T(128)}, f32[]{:T(128)}) all-reduce(f32[]{:T(128)} %get-tuple-element.39, f32[]{:T(128)} %get-tuple-element.40), channel_id=1, replica_groups=mesh['level'=2,'gx'=4,'yz'=4] {'gx'}, use_global_device_ids=true, to_apply=%region_38.39 | all-reduce | flops 2 | bytes 16 | tf_op jit(solution)/shard_map/psum | solution.py:49
  404.2 11.3 %all-reduce.42 = (f32[]{:T(128)}, f32[]{:T(128)}) all-reduce(f32[]{:T(128)} %get-tuple-element.14, f32[]{:T(128)} %get-tuple-element.13), channel_id=1, replica_groups=mesh['level'=2,'gx'=4,'yz'=4] {'yz'}, use_global_device_ids=true, to_apply=%region_43.44 | all-reduce | flops 2 | bytes 16 | tf_op jit(solution)/shard_map/psum | solution.py:50
  415.5 11.0 %all-reduce.54 = (f32[]{:T(128)}, f32[]{:T(128)}) all-reduce(f32[]{:T(128)} %get-tuple-element.37, f32[]{:T(128)} %get-tuple-element.38), channel_id=1, replica_groups=mesh['level'=2,'gx'=4,'yz'=4] {'gx'}, use_global_device_ids=true, to_apply=%region_44.45 | all-reduce | flops 2 | bytes 16 | tf_op jit(solution)/shard_map/psum | solution.py:49
  449.2 11.3 %all-reduce.41 = (f32[]{:T(128)}, f32[]{:T(128)}) all-reduce(f32[]{:T(128)} %get-tuple-element.12, f32[]{:T(128)} %get-tuple-element.11), channel_id=1, replica_groups=mesh['level'=2,'gx'=4,'yz'=4] {'yz'}, use_global_device_ids=true, to_apply=%region_49.50 | all-reduce | flops 2 | bytes 16 | tf_op jit(solution)/shard_map/psum | solution.py:50
  460.5 11.0 %all-reduce.53 = (f32[]{:T(128)}, f32[]{:T(128)}) all-reduce(f32[]{:T(128)} %get-tuple-element.35, f32[]{:T(128)} %get-tuple-element.36), channel_id=1, replica_groups=mesh['level'=2,'gx'=4,'yz'=4] {'gx'}, use_global_device_ids=true, to_apply=%region_50.51 | all-reduce | flops 2 | bytes 16 | tf_op jit(solution)/shard_map/psum | solution.py:49
  480.4 5.7 collective-permute-start.60
  501.8 5.4 collective-permute-start.68
  522.7 12.2 %all-reduce.40 = (f32[]{:T(128)}, f32[]{:T(128)}) all-reduce(f32[]{:T(128)} %get-tuple-element.10, f32[]{:T(128)} %get-tuple-element.9), channel_id=1, replica_groups=mesh['level'=2,'gx'=4,'yz'=4] {'yz'}, use_global_device_ids=true, to_apply=%region_55.56 | all-reduce | flops 2 | bytes 16 | tf_op jit(solution)/shard_map/psum | solution.py:50
  534.9 11.0 %all-reduce.52 = (f32[]{:T(128)}, f32[]{:T(128)}) all-reduce(f32[]{:T(128)} %get-tuple-element.33, f32[]{:T(128)} %get-tuple-element.34), channel_id=1, replica_groups=mesh['level'=2,'gx'=4,'yz'=4] {'gx'}, use_global_device_ids=true, to_apply=%region_56.57 | all-reduce | flops 2 | bytes 16 | tf_op jit(solution)/shard_map/psum | solution.py:49
  565.1 11.3 %all-reduce.39 = (f32[]{:T(128)}, f32[]{:T(128)}) all-reduce(f32[]{:T(128)} %get-tuple-element.8, f32[]{:T(128)} %get-tuple-element.7), channel_id=1, replica_groups=mesh['level'=2,'gx'=4,'yz'=4] {'yz'}, use_global_device_ids=true, to_apply=%region_61.62 | all-reduce | flops 2 | bytes 16 | tf_op jit(solution)/shard_map/psum | solution.py:50
  576.4 11.0 %all-reduce.51 = (f32[]{:T(128)}, f32[]{:T(128)}) all-reduce(f32[]{:T(128)} %get-tuple-element.31, f32[]{:T(128)} %get-tuple-element.32), channel_id=1, replica_groups=mesh['level'=2,'gx'=4,'yz'=4] {'gx'}, use_global_device_ids=true, to_apply=%region_62.63 | all-reduce | flops 2 | bytes 16 | tf_op jit(solution)/shard_map/psum | solution.py:49
  610.0 11.3 %all-reduce.38 = (f32[]{:T(128)}, f32[]{:T(128)}) all-reduce(f32[]{:T(128)} %get-tuple-element.6, f32[]{:T(128)} %get-tuple-element.5), channel_id=1, replica_groups=mesh['level'=2,'gx'=4,'yz'=4] {'yz'}, use_global_device_ids=true, to_apply=%region_67.68 | all-reduce | flops 2 | bytes 16 | tf_op jit(solution)/shard_map/psum | solution.py:50
  621.3 11.0 %all-reduce.50 = (f32[]{:T(128)}, f32[]{:T(128)}) all-reduce(f32[]{:T(128)} %get-tuple-element.29, f32[]{:T(128)} %get-tuple-element.30), channel_id=1, replica_groups=mesh['level'=2,'gx'=4,'yz'=4] {'gx'}, use_global_device_ids=true, to_apply=%region_68.69 | all-reduce | flops 2 | bytes 16 | tf_op jit(solution)/shard_map/psum | solution.py:49
  (261 shorter events, 282.0 us)
Async XLA Ops:
  110.4 6.8 %collective-permute-start.12 = (f32[1,16,256]{2,1,0:T(8,128)S(1)}, f32[1,16,256]{2,1,0:T(8,128)S(1)}, u32[]{:S(2)}, u32[]{:S(2)}) collective-permute-start(f32[1,16,256]{2,1,0:T(8,128)S(1)} %get-tuple-element.186), channel_id=1, source_target_pairs={{4,0},{8,4},{12,8},{5,1},{9,5},{13,9},{6,2},{10,6},{14,10},{7,3},{... | collective-permute-start | bytes 49160 | tf_op jit(solution)/shard_map/ppermute | solution.py:21
  153.5 11.0 %collective-permute-start.22 = (f32[1,16,256]{2,1,0:T(8,128)S(1)}, f32[1,16,256]{2,1,0:T(8,128)S(1)}, u32[]{:S(2)}, u32[]{:S(2)}) collective-permute-start(f32[1,16,256]{2,1,0:T(8,128)S(1)} %get-tuple-element.181), channel_id=1, source_target_pairs={{0,4},{4,8},{8,12},{1,5},{5,9},{9,13},{2,6},{6,10},{10,14},{3,7},{... | collective-permute-start | bytes 49160 | tf_op jit(solution)/shard_map/ppermute | solution.py:19
  155.1 9.3 %collective-permute-start.21 = (f32[1,16,256]{2,1,0:T(8,128)S(1)}, f32[1,16,256]{2,1,0:T(8,128)S(1)}, u32[]{:S(2)}, u32[]{:S(2)}) collective-permute-start(f32[1,16,256]{2,1,0:T(8,128)S(1)} %get-tuple-element.182), channel_id=1, source_target_pairs={{4,0},{8,4},{12,8},{5,1},{9,5},{13,9},{6,2},{10,6},{14,10},{7,3},{... | collective-permute-start | bytes 49160 | tf_op jit(solution)/shard_map/ppermute | solution.py:21
  157.5 12.9 %collective-permute-start.18 = (f32[1,16,256]{2,1,0:T(8,128)S(1)}, f32[1,16,256]{2,1,0:T(8,128)S(1)}, u32[]{:S(2)}, u32[]{:S(2)}) collective-permute-start(f32[1,16,256]{2,1,0:T(8,128)S(1)} %get-tuple-element.179), channel_id=1, source_target_pairs={{0,4},{4,8},{8,12},{1,5},{5,9},{9,13},{2,6},{6,10},{10,14},{3,7},{... | collective-permute-start | bytes 49160 | tf_op jit(solution)/shard_map/ppermute | solution.py:19
  163.2 7.2 %collective-permute-start.17 = (f32[1,16,256]{2,1,0:T(8,128)S(1)}, f32[1,16,256]{2,1,0:T(8,128)S(1)}, u32[]{:S(2)}, u32[]{:S(2)}) collective-permute-start(f32[1,16,256]{2,1,0:T(8,128)S(1)} %get-tuple-element.180), channel_id=1, source_target_pairs={{4,0},{8,4},{12,8},{5,1},{9,5},{13,9},{6,2},{10,6},{14,10},{7,3},{... | collective-permute-start | bytes 49160 | tf_op jit(solution)/shard_map/ppermute | solution.py:21
  164.6 12.2 %collective-permute-start.23 = (f32[34,1,256]{2,1,0:T(1,128)S(1)}, f32[34,1,256]{2,1,0:T(1,128)S(1)}, u32[]{:S(2)}, u32[]{:S(2)}) collective-permute-start(f32[34,1,256]{2,1,0:T(1,128)S(1)} %get-tuple-element.113), channel_id=1, source_target_pairs={{1,0},{2,1},{3,2},{5,4},{6,5},{7,6},{9,8},{10,9},{11,10},{13,12},{... | collective-permute-start | bytes 104456 | tf_op jit(solution)/shard_map/ppermute | solution.py:21
  165.9 10.9 %collective-permute-start.24 = (f32[34,1,256]{2,1,0:T(1,128)S(1)}, f32[34,1,256]{2,1,0:T(1,128)S(1)}, u32[]{:S(2)}, u32[]{:S(2)}) collective-permute-start(f32[34,1,256]{2,1,0:T(1,128)S(1)} %get-tuple-element.114), channel_id=1, source_target_pairs={{0,1},{1,2},{2,3},{4,5},{5,6},{6,7},{8,9},{9,10},{10,11},{12,13},{... | collective-permute-start | bytes 104456 | tf_op jit(solution)/shard_map/ppermute | solution.py:19
  178.9 6.9 %collective-permute-start.26 = (f32[1,16,256]{2,1,0:T(8,128)S(1)}, f32[1,16,256]{2,1,0:T(8,128)S(1)}, u32[]{:S(2)}, u32[]{:S(2)}) collective-permute-start(f32[1,16,256]{2,1,0:T(8,128)S(1)} %get-tuple-element.171), channel_id=1, source_target_pairs={{0,4},{4,8},{8,12},{1,5},{5,9},{9,13},{2,6},{6,10},{10,14},{3,7},{... | collective-permute-start | bytes 49160 | tf_op jit(solution)/shard_map/ppermute | solution.py:19
  184.4 6.5 %collective-permute-start.25 = (f32[1,16,256]{2,1,0:T(8,128)S(1)}, f32[1,16,256]{2,1,0:T(8,128)S(1)}, u32[]{:S(2)}, u32[]{:S(2)}) collective-permute-start(f32[1,16,256]{2,1,0:T(8,128)S(1)} %get-tuple-element.172), channel_id=1, source_target_pairs={{4,0},{8,4},{12,8},{5,1},{9,5},{13,9},{6,2},{10,6},{14,10},{7,3},{... | collective-permute-start | bytes 49160 | tf_op jit(solution)/shard_map/ppermute | solution.py:21
  226.1 6.8 %collective-permute-start.29 = (f32[1,16,256]{2,1,0:T(8,128)S(1)}, f32[1,16,256]{2,1,0:T(8,128)S(1)}, u32[]{:S(2)}, u32[]{:S(2)}) collective-permute-start(f32[1,16,256]{2,1,0:T(8,128)S(1)} %get-tuple-element.168), channel_id=1, source_target_pairs={{4,0},{8,4},{12,8},{5,1},{9,5},{13,9},{6,2},{10,6},{14,10},{7,3},{... | collective-permute-start | bytes 49160 | tf_op jit(solution)/shard_map/ppermute | solution.py:21
  271.8 6.8 %collective-permute-start.33 = (f32[1,16,256]{2,1,0:T(8,128)S(1)}, f32[1,16,256]{2,1,0:T(8,128)S(1)}, u32[]{:S(2)}, u32[]{:S(2)}) collective-permute-start(f32[1,16,256]{2,1,0:T(8,128)S(1)} %get-tuple-element.166), channel_id=1, source_target_pairs={{4,0},{8,4},{12,8},{5,1},{9,5},{13,9},{6,2},{10,6},{14,10},{7,3},{... | collective-permute-start | bytes 49160 | tf_op jit(solution)/shard_map/ppermute | solution.py:21
  315.1 11.3 %collective-permute-start.43 = (f32[1,16,256]{2,1,0:T(8,128)S(1)}, f32[1,16,256]{2,1,0:T(8,128)S(1)}, u32[]{:S(2)}, u32[]{:S(2)}) collective-permute-start(f32[1,16,256]{2,1,0:T(8,128)S(1)} %get-tuple-element.161), channel_id=1, source_target_pairs={{0,4},{4,8},{8,12},{1,5},{5,9},{9,13},{2,6},{6,10},{10,14},{3,7},{... | collective-permute-start | bytes 49160 | tf_op jit(solution)/shard_map/ppermute | solution.py:19
  316.7 9.7 %collective-permute-start.42 = (f32[1,16,256]{2,1,0:T(8,128)S(1)}, f32[1,16,256]{2,1,0:T(8,128)S(1)}, u32[]{:S(2)}, u32[]{:S(2)}) collective-permute-start(f32[1,16,256]{2,1,0:T(8,128)S(1)} %get-tuple-element.162), channel_id=1, source_target_pairs={{4,0},{8,4},{12,8},{5,1},{9,5},{13,9},{6,2},{10,6},{14,10},{7,3},{... | collective-permute-start | bytes 49160 | tf_op jit(solution)/shard_map/ppermute | solution.py:21
  319.2 13.1 %collective-permute-start.39 = (f32[1,16,256]{2,1,0:T(8,128)S(1)}, f32[1,16,256]{2,1,0:T(8,128)S(1)}, u32[]{:S(2)}, u32[]{:S(2)}) collective-permute-start(f32[1,16,256]{2,1,0:T(8,128)S(1)} %get-tuple-element.159), channel_id=1, source_target_pairs={{0,4},{4,8},{8,12},{1,5},{5,9},{9,13},{2,6},{6,10},{10,14},{3,7},{... | collective-permute-start | bytes 49160 | tf_op jit(solution)/shard_map/ppermute | solution.py:19
  324.9 7.4 %collective-permute-start.38 = (f32[1,16,256]{2,1,0:T(8,128)S(1)}, f32[1,16,256]{2,1,0:T(8,128)S(1)}, u32[]{:S(2)}, u32[]{:S(2)}) collective-permute-start(f32[1,16,256]{2,1,0:T(8,128)S(1)} %get-tuple-element.160), channel_id=1, source_target_pairs={{4,0},{8,4},{12,8},{5,1},{9,5},{13,9},{6,2},{10,6},{14,10},{7,3},{... | collective-permute-start | bytes 49160 | tf_op jit(solution)/shard_map/ppermute | solution.py:21
  326.5 12.2 %collective-permute-start.44 = (f32[34,1,256]{2,1,0:T(1,128)S(1)}, f32[34,1,256]{2,1,0:T(1,128)S(1)}, u32[]{:S(2)}, u32[]{:S(2)}) collective-permute-start(f32[34,1,256]{2,1,0:T(1,128)S(1)} %get-tuple-element.103), channel_id=1, source_target_pairs={{1,0},{2,1},{3,2},{5,4},{6,5},{7,6},{9,8},{10,9},{11,10},{13,12},{... | collective-permute-start | bytes 104456 | tf_op jit(solution)/shard_map/ppermute | solution.py:21
  327.8 10.9 %collective-permute-start.45 = (f32[34,1,256]{2,1,0:T(1,128)S(1)}, f32[34,1,256]{2,1,0:T(1,128)S(1)}, u32[]{:S(2)}, u32[]{:S(2)}) collective-permute-start(f32[34,1,256]{2,1,0:T(1,128)S(1)} %get-tuple-element.104), channel_id=1, source_target_pairs={{0,1},{1,2},{2,3},{4,5},{5,6},{6,7},{8,9},{9,10},{10,11},{12,13},{... | collective-permute-start | bytes 104456 | tf_op jit(solution)/shard_map/ppermute | solution.py:19
  340.8 6.9 %collective-permute-start.47 = (f32[1,16,256]{2,1,0:T(8,128)S(1)}, f32[1,16,256]{2,1,0:T(8,128)S(1)}, u32[]{:S(2)}, u32[]{:S(2)}) collective-permute-start(f32[1,16,256]{2,1,0:T(8,128)S(1)} %get-tuple-element.151), channel_id=1, source_target_pairs={{0,4},{4,8},{8,12},{1,5},{5,9},{9,13},{2,6},{6,10},{10,14},{3,7},{... | collective-permute-start | bytes 49160 | tf_op jit(solution)/shard_map/ppermute | solution.py:19
  346.3 6.5 %collective-permute-start.46 = (f32[1,16,256]{2,1,0:T(8,128)S(1)}, f32[1,16,256]{2,1,0:T(8,128)S(1)}, u32[]{:S(2)}, u32[]{:S(2)}) collective-permute-start(f32[1,16,256]{2,1,0:T(8,128)S(1)} %get-tuple-element.152), channel_id=1, source_target_pairs={{4,0},{8,4},{12,8},{5,1},{9,5},{13,9},{6,2},{10,6},{14,10},{7,3},{... | collective-permute-start | bytes 49160 | tf_op jit(solution)/shard_map/ppermute | solution.py:21
  388.0 6.8 %collective-permute-start.50 = (f32[1,16,256]{2,1,0:T(8,128)S(1)}, f32[1,16,256]{2,1,0:T(8,128)S(1)}, u32[]{:S(2)}, u32[]{:S(2)}) collective-permute-start(f32[1,16,256]{2,1,0:T(8,128)S(1)} %get-tuple-element.148), channel_id=1, source_target_pairs={{4,0},{8,4},{12,8},{5,1},{9,5},{13,9},{6,2},{10,6},{14,10},{7,3},{... | collective-permute-start | bytes 49160 | tf_op jit(solution)/shard_map/ppermute | solution.py:21
  433.8 6.8 %collective-permute-start.54 = (f32[1,16,256]{2,1,0:T(8,128)S(1)}, f32[1,16,256]{2,1,0:T(8,128)S(1)}, u32[]{:S(2)}, u32[]{:S(2)}) collective-permute-start(f32[1,16,256]{2,1,0:T(8,128)S(1)} %get-tuple-element.146), channel_id=1, source_target_pairs={{4,0},{8,4},{12,8},{5,1},{9,5},{13,9},{6,2},{10,6},{14,10},{7,3},{... | collective-permute-start | bytes 49160 | tf_op jit(solution)/shard_map/ppermute | solution.py:21
  477.0 10.5 %collective-permute-start.64 = (f32[1,16,256]{2,1,0:T(8,128)S(1)}, f32[1,16,256]{2,1,0:T(8,128)S(1)}, u32[]{:S(2)}, u32[]{:S(2)}) collective-permute-start(f32[1,16,256]{2,1,0:T(8,128)S(1)} %get-tuple-element.141), channel_id=1, source_target_pairs={{0,4},{4,8},{8,12},{1,5},{5,9},{9,13},{2,6},{6,10},{10,14},{3,7},{... | collective-permute-start | bytes 49160 | tf_op jit(solution)/shard_map/ppermute | solution.py:19
  478.6 8.8 %collective-permute-start.63 = (f32[1,16,256]{2,1,0:T(8,128)S(1)}, f32[1,16,256]{2,1,0:T(8,128)S(1)}, u32[]{:S(2)}, u32[]{:S(2)}) collective-permute-start(f32[1,16,256]{2,1,0:T(8,128)S(1)} %get-tuple-element.142), channel_id=1, source_target_pairs={{4,0},{8,4},{12,8},{5,1},{9,5},{13,9},{6,2},{10,6},{14,10},{7,3},{... | collective-permute-start | bytes 49160 | tf_op jit(solution)/shard_map/ppermute | solution.py:21
  480.4 13.0 %collective-permute-start.60 = (f32[1,16,256]{2,1,0:T(8,128)S(1)}, f32[1,16,256]{2,1,0:T(8,128)S(1)}, u32[]{:S(2)}, u32[]{:S(2)}) collective-permute-start(f32[1,16,256]{2,1,0:T(8,128)S(1)} %get-tuple-element.139), channel_id=1, source_target_pairs={{0,4},{4,8},{8,12},{1,5},{5,9},{9,13},{2,6},{6,10},{10,14},{3,7},{... | collective-permute-start | bytes 49160 | tf_op jit(solution)/shard_map/ppermute | solution.py:19
  486.1 7.2 %collective-permute-start.59 = (f32[1,16,256]{2,1,0:T(8,128)S(1)}, f32[1,16,256]{2,1,0:T(8,128)S(1)}, u32[]{:S(2)}, u32[]{:S(2)}) collective-permute-start(f32[1,16,256]{2,1,0:T(8,128)S(1)} %get-tuple-element.140), channel_id=1, source_target_pairs={{4,0},{8,4},{12,8},{5,1},{9,5},{13,9},{6,2},{10,6},{14,10},{7,3},{... | collective-permute-start | bytes 49160 | tf_op jit(solution)/shard_map/ppermute | solution.py:21
  487.5 12.2 %collective-permute-start.65 = (f32[34,1,256]{2,1,0:T(1,128)S(1)}, f32[34,1,256]{2,1,0:T(1,128)S(1)}, u32[]{:S(2)}, u32[]{:S(2)}) collective-permute-start(f32[34,1,256]{2,1,0:T(1,128)S(1)} %get-tuple-element.93), channel_id=1, source_target_pairs={{1,0},{2,1},{3,2},{5,4},{6,5},{7,6},{9,8},{10,9},{11,10},{13,12},{... | collective-permute-start | bytes 104456 | tf_op jit(solution)/shard_map/ppermute | solution.py:21
  488.8 10.9 %collective-permute-start.66 = (f32[34,1,256]{2,1,0:T(1,128)S(1)}, f32[34,1,256]{2,1,0:T(1,128)S(1)}, u32[]{:S(2)}, u32[]{:S(2)}) collective-permute-start(f32[34,1,256]{2,1,0:T(1,128)S(1)} %get-tuple-element.94), channel_id=1, source_target_pairs={{0,1},{1,2},{2,3},{4,5},{5,6},{6,7},{8,9},{9,10},{10,11},{12,13},{... | collective-permute-start | bytes 104456 | tf_op jit(solution)/shard_map/ppermute | solution.py:19
  501.8 6.9 %collective-permute-start.68 = (f32[1,16,256]{2,1,0:T(8,128)S(1)}, f32[1,16,256]{2,1,0:T(8,128)S(1)}, u32[]{:S(2)}, u32[]{:S(2)}) collective-permute-start(f32[1,16,256]{2,1,0:T(8,128)S(1)} %get-tuple-element.131), channel_id=1, source_target_pairs={{0,4},{4,8},{8,12},{1,5},{5,9},{9,13},{2,6},{6,10},{10,14},{3,7},{... | collective-permute-start | bytes 49160 | tf_op jit(solution)/shard_map/ppermute | solution.py:19
  507.3 6.5 %collective-permute-start.67 = (f32[1,16,256]{2,1,0:T(8,128)S(1)}, f32[1,16,256]{2,1,0:T(8,128)S(1)}, u32[]{:S(2)}, u32[]{:S(2)}) collective-permute-start(f32[1,16,256]{2,1,0:T(8,128)S(1)} %get-tuple-element.132), channel_id=1, source_target_pairs={{4,0},{8,4},{12,8},{5,1},{9,5},{13,9},{6,2},{10,6},{14,10},{7,3},{... | collective-permute-start | bytes 49160 | tf_op jit(solution)/shard_map/ppermute | solution.py:21
  515.2 6.5 %collective-permute-start.70 = (f32[34,1,256]{2,1,0:T(1,128)S(1)}, f32[34,1,256]{2,1,0:T(1,128)S(1)}, u32[]{:S(2)}, u32[]{:S(2)}) collective-permute-start(f32[34,1,256]{2,1,0:T(1,128)S(1)} %get-tuple-element.90), channel_id=1, source_target_pairs={{0,1},{1,2},{2,3},{4,5},{5,6},{6,7},{8,9},{9,10},{10,11},{12,13},{... | collective-permute-start | bytes 104456 | tf_op jit(solution)/shard_map/ppermute | solution.py:19
  548.9 6.8 %collective-permute-start.71 = (f32[1,16,256]{2,1,0:T(8,128)S(1)}, f32[1,16,256]{2,1,0:T(8,128)S(1)}, u32[]{:S(2)}, u32[]{:S(2)}) collective-permute-start(f32[1,16,256]{2,1,0:T(8,128)S(1)} %get-tuple-element.128), channel_id=1, source_target_pairs={{4,0},{8,4},{12,8},{5,1},{9,5},{13,9},{6,2},{10,6},{14,10},{7,3},{... | collective-permute-start | bytes 49160 | tf_op jit(solution)/shard_map/ppermute | solution.py:21
  594.7 6.8 %collective-permute-start.75 = (f32[1,16,256]{2,1,0:T(8,128)S(1)}, f32[1,16,256]{2,1,0:T(8,128)S(1)}, u32[]{:S(2)}, u32[]{:S(2)}) collective-permute-start(f32[1,16,256]{2,1,0:T(8,128)S(1)} %get-tuple-element.126), channel_id=1, source_target_pairs={{4,0},{8,4},{12,8},{5,1},{9,5},{13,9},{6,2},{10,6},{14,10},{7,3},{... | collective-permute-start | bytes 49160 | tf_op jit(solution)/shard_map/ppermute | solution.py:21
  (57 other events, 308.0 us)
